TPU v7x, 128 devices: a whole 4x4x4 slice. The times are simulated.
128 devices in a mesh: node: 32 (over x, z, core), local: 4 (over y).
Axes of the slice: x: 4, y: 4, z: 4, core: 2. Of those that a mesh axis runs over, the one named last changes fastest.
Arguments:
- tokens: bfloat16 [8192, 5120], P(('node', 'local')), may hold values from -6 to 6
- node_ids: int32 [8192, 3], P(('node', 'local')), may hold values from 0 to 31, as said below
- expert_ids: int32 [8192, 6], P(('node', 'local')), may hold values from 0 to 95, as said below
- gate_weights: bfloat16 [8192, 6], P(('node', 'local')), may hold values from 0.049804688 to 1
- up_weight: bfloat16 [96, 5120, 1536], P('node', None, 'local'), may hold values from -0.078125 to 0.078125
- down_weight: bfloat16 [96, 1536, 5120], P('node', 'local'), may hold values from -0.15625 to 0.15625
Outputs:
- routed_out: bfloat16 [8192, 5120], P(('node', 'local'))
Inputs may be any that keep to these rules, and one draw needn't show every extreme that they name: `node_ids`: each token names 3 different nodes; the 64 tokens of one device name every node exactly 6 times. Node m holds experts 3 * m to 3 * m + 2. For each j, expert_ids[t, 2 * j] and expert_ids[t, 2 * j + 1] are two different experts of node node_ids[t, j].
All inputs are finite; a program needn't handle non-finite values.
Results may differ from a plain program's by a relative error of at most 0.012.
Values may be sent and summed in bfloat16 or wider, within the bound.
A program may use at most 192 MiB of HBM per device.

v0:
```python
import jax
import jax.numpy as jnp
from jax import lax
from jax.sharding import PartitionSpec as P


def body(tokens, node_ids, expert_ids, gate_weights, up_weight, down_weight):
    tok_rows, model_width = tokens.shape
    node_count = lax.axis_size("node")
    per_node = up_weight.shape[0]
    capacity = node_ids.shape[1] * tok_rows // node_count
    slot_count = node_count * capacity
    node_grid = jnp.arange(node_count, dtype=jnp.int32)
    picked = jnp.any(node_ids[:, :, None] == node_grid[None, None, :], axis=1).astype(jnp.int32)
    rank_rows = jnp.cumsum(picked, axis=0) - picked
    target = jnp.where(picked > 0, node_grid[None, :] * capacity + rank_rows, -1)
    slot_grid = jnp.arange(slot_count, dtype=jnp.int32)
    placing = (jnp.repeat(target, capacity, axis=1) == slot_grid[None, :]).astype(jnp.bfloat16)
    expert_grid = jnp.arange(node_count * per_node, dtype=jnp.int32)
    flat_gates = jnp.sum(
        jnp.where(
            expert_ids[:, :, None] == expert_grid[None, None, :],
            gate_weights.astype(jnp.float32)[:, :, None],
            0.0,
        ),
        axis=1,
    )
    by_node = jnp.repeat(flat_gates.reshape(tok_rows, node_count, per_node), capacity, axis=1)
    slot_gates = jnp.einsum("ts,tse->se", placing.astype(jnp.float32), by_node)
    outgoing = lax.dot_general(
        placing, tokens, (((0,), (0,)), ((), ())), preferred_element_type=jnp.float32
    ).astype(jnp.bfloat16)
    arrived, arrived_gates = (
        lax.all_to_all(
            outgoing.reshape(node_count, capacity, model_width),
            "node",
            split_axis=0,
            concat_axis=0,
            tiled=True,
        ),
        lax.all_to_all(
            slot_gates.astype(jnp.bfloat16).reshape(node_count, capacity, per_node),
            "node",
            split_axis=0,
            concat_axis=0,
            tiled=True,
        ),
    )
    arrived = arrived.reshape(slot_count, model_width)
    arrived_gates = arrived_gates.reshape(slot_count, per_node)
    pooled, pooled_gates = (
        lax.all_gather(arrived, "local", axis=0, tiled=True),
        lax.all_gather(arrived_gates, "local", axis=0, tiled=True),
    )
    rows_gate = pooled_gates.astype(jnp.float32)
    running = jnp.zeros((slot_count * lax.axis_size("local"), model_width), jnp.float32)
    for expert in range(per_node):
        lifted = jnp.dot(pooled, up_weight[expert], preferred_element_type=jnp.float32)
        scaled = (jax.nn.silu(lifted) * rows_gate[:, expert : expert + 1]).astype(jnp.bfloat16)
        running = running + jnp.dot(scaled, down_weight[expert], preferred_element_type=jnp.float32)
    summed = lax.psum_scatter(
        running.astype(jnp.bfloat16).astype(jnp.float32).astype(jnp.bfloat16),
        "local",
        scatter_dimension=0,
        tiled=True,
    )
    returned = lax.all_to_all(
        summed.reshape(node_count, capacity, model_width),
        "node",
        split_axis=0,
        concat_axis=0,
        tiled=True,
    )
    combined = jnp.dot(
        placing, returned.reshape(slot_count, model_width), preferred_element_type=jnp.float32
    )
    return combined.astype(jnp.bfloat16)


def solution(mesh):
    in_specs = (
        P(("node", "local"), None),
        P(("node", "local"), None),
        P(("node", "local"), None),
        P(("node", "local"), None),
        P("node", None, "local"),
        P("node", "local", None),
    )
    out_specs = P(("node", "local"), None)
    return jax.shard_map(body, mesh=mesh, in_specs=in_specs, out_specs=out_specs, check_vma=False)
```

profile of v0, /device:TPU:1, one launch (start us, length us, event | category | flops | bytes accessed | tf_op | source)
XLA Modules:
  0.0 324.2 jit_solution(444758490590789714)
XLA Ops:
  6.5 0.0 copy-start
  6.5 0.8 fusion.40
  7.3 0.1 copy.46
  7.4 0.1 reduce_window_sum.11
  7.5 0.1 copy.47
  7.6 1.9 convolution_convert_fusion
  9.6 2.6 reshape.44
  12.2 43.4 %all_to_all.15 = bf16[32,6,5120]{2,1,0:T(8,128)(2,1)} all-to-all(bf16[32,6,5120]{2,1,0:T(8,128)(2,1)S(1)} %reshape.44), channel_id=1, replica_groups=mesh['node'=32,'local'=4] {'node'}, dimensions={0} | all-to-all | bytes 3932160 | tf_op jit(solution)/shard_map/all_to_all | solution.py:34
  55.6 4.2 %reshape.45 = bf16[192,5120]{1,0:T(8,128)(2,1)} reshape(bf16[32,6,5120]{2,1,0:T(8,128)(2,1)} %all_to_all.15) | data formatting | bytes 3932160 | tf_op jit(solution)/shard_map/reshape | solution.py:49
  59.8 0.0 all-gather.3.cloned.1.call-update
  59.8 0.0 reduce-scatter.2.cloned.1.call-start
  59.9 0.2 select_reduce_fusion
  60.1 0.1 copy.48
  60.2 0.1 broadcast_in_dim.33.clone
  60.3 0.3 fusion.37
  60.7 0.1 copy.57
  60.7 0.1 reshape.48
  60.9 10.7 %all_to_all.16 = bf16[32,6,3]{1,2,0:T(4,128)(2,1)S(1)} all-to-all(bf16[32,6,3]{1,2,0:T(4,128)(2,1)S(1)} %copy.50), channel_id=1, replica_groups=mesh['node'=32,'local'=4] {'node'}, dimensions={0} | all-to-all | bytes 2304 | tf_op jit(solution)/shard_map/all_to_all | solution.py:41
  71.6 0.1 reshape.51
  71.7 10.3 %all-gather = bf16[4,192,3]{1,2,0:T(4,128)(2,1)S(1)} all-gather(bf16[1,192,3]{1,2,0:T(4,128)(2,1)S(1)} %reshape.51), channel_id=1, replica_groups=mesh['node'=32,'local'=4] {'local'}, dimensions={0}, use_global_device_ids=true | all-gather | bytes 5760 | tf_op jit(solution)/shard_map/all_gather | solution.py:53
  82.0 0.1 reshape.53
  82.2 53.9 %all-gather.3.cloned.1.call-done = bf16[768,5120]{1,0:T(8,128)(2,1)} async-done(((bf16[192,5120]{1,0:T(8,128)(2,1)}), bf16[768,5120]{1,0:T(8,128)(2,1)}) %all-gather.3.cloned.1.call-update) | async-done | bytes 7864336 | tf_op jit(solution)/shard_map/all_gather | solution.py:52
  136.1 16.3 %fusion.4 = f32[768,5120]{1,0:T(8,128)} fusion(bf16[3,384,5120]{2,1,0:T(8,128)(2,1)} %param.11, bf16[768,5120]{1,0:T(8,128)(2,1)} %all-gather.3.cloned.1.call-done, bf16[3,5120,384]{2,1,0:T(8,128)(2,1)} %param.10, f32[768]{0:T(1024)S(1)} %get-tuple-element.6), kind=kOutput, calls=%fused_computation.7 | convolution fusion | flops 6041567232 | bytes 31460352 | tf_op jit(solution)/shard_map/dot_general | solution.py:60
  152.3 16.3 %fusion.8 = f32[768,5120]{1,0:T(8,128)} fusion(bf16[3,384,5120]{2,1,0:T(8,128)(2,1)} %param.11, bf16[768,5120]{1,0:T(8,128)(2,1)} %all-gather.3.cloned.1.call-done, bf16[3,5120,384]{2,1,0:T(8,128)(2,1)} %param.10, f32[768]{0:T(1024)S(1)} %get-tuple-element.7), kind=kOutput, calls=%fused_computation.11 | convolution fusion | flops 6041567232 | bytes 31460352 | tf_op jit(solution)/shard_map/dot_general | solution.py:60
  168.6 22.9 %add_convert_fusion = bf16[768,5120]{1,0:T(8,128)(2,1)} fusion(f32[768,5120]{1,0:T(8,128)} %fusion.8, f32[768,5120]{1,0:T(8,128)} %fusion.4, bf16[3,384,5120]{2,1,0:T(8,128)(2,1)} %param.11, bf16[768,5120]{1,0:T(8,128)(2,1)} %all-gather.3.cloned.1.call-done, bf16[3,5120,384]{2,1,0:T(8,128)(2,1)} %param.10, f32[768]{0:T(1024)S(1)} %get-tuple-element.5), kind=kOutput, calls=%fused_computation | convolution fusion | flops 6053363712 | bytes 55053312 | tf_op jit(solution)/shard_map/dot_general | solution.py:60
  191.5 0.0 reduce-scatter.2.cloned.1.call-update
  191.5 77.8 %reduce-scatter.2.cloned.1.call-done = bf16[192,5120]{1,0:T(8,128)(2,1)} async-done(((bf16[768,5120]{1,0:T(8,128)(2,1)}), bf16[192,5120]{1,0:T(8,128)(2,1)}) %reduce-scatter.2.cloned.1.call-update) | async-done | bytes 1966096 | tf_op jit(solution)/shard_map/reduce_scatter | solution.py:61
  269.4 4.2 %reshape.50 = bf16[32,6,5120]{2,1,0:T(8,128)(2,1)} reshape(bf16[192,5120]{1,0:T(8,128)(2,1)} %reduce-scatter.2.cloned.1.call-done) | data formatting | bytes 3932160 | tf_op jit(solution)/shard_map/reshape | solution.py:68
  273.5 7.7 %all-to-all-start.2 = ((bf16[32,6,5120]{2,1,0:T(8,128)(2,1)}), bf16[32,6,5120]{2,1,0:T(8,128)(2,1)S(1)}, u32[]{:S(2)}, u32[]{:S(2)}) async-start(bf16[32,6,5120]{2,1,0:T(8,128)(2,1)} %reshape.50), calls=%async_computation.3 | async-start | bytes 5242880 | tf_op jit(solution)/shard_map/all_to_all | solution.py:67
  281.3 0.1 broadcast_compare_fusion
  281.4 33.8 %all-to-all-done.2 = bf16[32,6,5120]{2,1,0:T(8,128)(2,1)S(1)} async-done(((bf16[32,6,5120]{2,1,0:T(8,128)(2,1)}), bf16[32,6,5120]{2,1,0:T(8,128)(2,1)S(1)}, u32[]{:S(2)}, u32[]{:S(2)}) %all-to-all-start.2) | async-done | bytes 1966112 | tf_op jit(solution)/shard_map/all_to_all | solution.py:67
  315.2 2.1 fusion
  (21 shorter events, 0.2 us)
Async XLA Ops:
  6.5 1.1 copy-start
  6.5 129.5 %all-gather.3.cloned.1.call-start = ((), (), s32[]{:S(2)}) async-start(), calls=%async_computation.4 | async-start | bytes 9830400 | tf_op jit(solution)/shard_map/all_gather | solution.py:52
  55.6 4.2 %copy-start.3 = (bf16[64,6]{0,1:T(8,128)(2,1)S(1)}, bf16[64,6]{0,1:T(8,128)(2,1)}, u32[]{:S(2)}) copy-start(bf16[64,6]{0,1:T(8,128)(2,1)} %param.9) | copy-start | bytes 2308
  55.6 4.3 %copy-start.2 = (s32[64,6]{0,1:T(8,128)S(1)}, s32[64,6]{0,1:T(8,128)}, u32[]{:S(2)}) copy-start(s32[64,6]{0,1:T(8,128)} %param.8) | copy-start | bytes 4612
  59.8 209.5 %reduce-scatter.2.cloned.1.call-start = ((), (), s32[]{:S(2)}) async-start(), calls=%async_computation.5 | async-start | bytes 9830400 | tf_op jit(solution)/shard_map/reduce_scatter | solution.py:61
  269.3 48.0 %copy-start.1 = (bf16[64,5120]{1,0:T(8,128)(2,1)S(1)}, bf16[64,5120]{1,0:T(8,128)(2,1)}, u32[]{:S(2)}) copy-start(bf16[64,5120]{1,0:T(8,128)(2,1)} %param.6) | copy-start | bytes 1966084
  273.5 41.7 %all-to-all-start.2 = ((bf16[32,6,5120]{2,1,0:T(8,128)(2,1)}), bf16[32,6,5120]{2,1,0:T(8,128)(2,1)S(1)}, u32[]{:S(2)}, u32[]{:S(2)}) async-start(bf16[32,6,5120]{2,1,0:T(8,128)(2,1)} %reshape.50), calls=%async_computation.3 | async-start | bytes 5242880 | tf_op jit(solution)/shard_map/all_to_all | solution.py:67
Sparse Core Ops, SparseCore 0:
  59.9 76.0 all-gather.2
  191.6 77.6 reduce-scatter.1
where the time goes:
time: 325 us; the launch traced here: 324 us
  waiting for transfers between devices  166 us (51%)
  blocking collectives  64.4 us (20%)
  matrix products  59.9 us (18%)
  between operations  13.6 us (4%)
  local copies, waits for them, and re-layouts  11.9 us (4%)
  starting transfers between devices  7.77 us (2%)
    reduce_scatter x1, waiting for transfers between devices, body(): lax.psum_scatter(running.astype(jnp.bfloat16).astype(jnp.float32).astype(...  77.8 us
    dot_general x3, matrix products, body(): jnp.dot(scaled, down_weight[expert], preferred_element_type=jnp.float32)  55.4 us
    all_gather x1, waiting for transfers between devices, body(): lax.all_gather(arrived, 'local', axis=0, tiled=True)  53.9 us
    all_to_all x1, blocking collectives, body(): lax.all_to_all(outgoing.reshape(node_count, capacity, model_width), 'node...  43.4 us
    all_to_all x1, waiting for transfers between devices, body(): lax.all_to_all(summed.reshape(node_count, capacity, model_width), 'node',...  33.8 us
    all_to_all x1, blocking collectives, body(): lax.all_to_all(slot_gates.astype(jnp.bfloat16).reshape(node_count, capaci...  10.7 us
    all_gather x1, blocking collectives, body(): lax.all_gather(arrived_gates, 'local', axis=0, tiled=True)  10.3 us
    all_to_all x1, starting transfers between devices, body(): lax.all_to_all(summed.reshape(node_count, capacity, model_width), 'node',...  7.73 us
  transfers between devices with their start and end apart: 3, of which 3 were waited for; matrix products, arithmetic and copies ran while one was open for 0% of the time, Pallas kernels for 0%

commit v1 on v0

v1 whole, which is shorter than its diff:
```python
import functools

import jax
import jax.numpy as jnp
from jax import lax
from jax.experimental import pallas as pl
from jax.experimental.pallas import tpu as pltpu
from jax.sharding import PartitionSpec as P

SLICE = 768
F32 = jnp.float32
BF16 = jnp.bfloat16


def kernel(cfg, tok, nid, eid, gw, up, down, out, *scr):
    n_node, n_loc, cap, n_exp, tr, d_model, ff, a, b = cfg
    (tA, ya, yb, ym, sel, selT, sendA, sendB, xa, xb, upv, dnv, hs, pa, pb, r1d, r1u, r2d, r2u, acc, retA, retB, fA, fB, oA, oB,
     tok_sem, w_sem, y_s, y_r, a_s, a_r, b_s, b_r, ag_s, ag_r, rs_s, rs_r, ra_s, ra_r, rb_s, rb_r, f_s, f_r) = scr
    rows = tr * 8
    cpn = n_loc * cap // 8
    blk = cpn * 8
    slots = n_node * blk
    ng = 4
    gn = n_node // ng
    gc = gn * cpn
    gr = gn * blk
    half = a // 2
    toks = n_loc * rows

    me = lax.axis_index("node")
    y = lax.axis_index("local")
    mx = me // gn
    yu = lax.rem(y + 1, n_loc)
    yd = lax.rem(y + n_loc - 1, n_loc)
    yo = lax.rem(y + 2, n_loc)

    def ncopy(src, dst, ss, rs, m):
        return pltpu.make_async_remote_copy(src, dst, ss, rs, device_id={"node": m}, device_id_type=pl.DeviceIdType.MESH)

    def ycopy(src, dst, ss, rs, p):
        return pltpu.make_async_remote_copy(src, dst, ss, rs, device_id={"local": p}, device_id_type=pl.DeviceIdType.MESH)

    barrier = pltpu.get_barrier_semaphore()

    @pl.loop(1, n_node)
    def _(d):
        pl.semaphore_signal(barrier, 1, device_id={"node": lax.rem(me + d, n_node)}, device_id_type=pl.DeviceIdType.MESH)

    @pl.loop(1, n_loc)
    def _(d):
        pl.semaphore_signal(barrier, 1, device_id={"local": lax.rem(y + d, n_loc)}, device_id_type=pl.DeviceIdType.MESH)

    def tok_copies():
        cs = [pltpu.make_async_copy(tok.at[:, :, pl.ds(s * a, a)], tA.at[s], tok_sem.at[s]) for s in range(n_loc)]
        cs.append(pltpu.make_async_copy(tok.at[:, :, pl.ds(pl.multiple_of(y * a, 128), a)], ya.at[y], tok_sem.at[n_loc]))
        cs.append(pltpu.make_async_copy(tok.at[:, :, pl.ds(n_loc * a, b)], yb.at[y], tok_sem.at[n_loc + 1]))
        return cs

    tcs = tok_copies()
    for c in tcs:
        c.start()
    ws = []
    for e in range(n_exp):
        ws.append(pltpu.make_async_copy(up.at[e], upv.at[:, pl.ds(e * ff, ff)], w_sem.at[e]))
        ws.append(pltpu.make_async_copy(down.at[e], dnv.at[pl.ds(e * ff, ff), :], w_sem.at[n_exp + e]))

    lane = lax.broadcasted_iota(jnp.int32, (rows, 128), 1)
    picked = jnp.zeros((rows, 128), F32)
    for k in range(nid.shape[1]):
        picked = jnp.where(nid[:, k : k + 1] == lane, 1.0, picked)
    gates = jnp.zeros((rows, 128), F32)
    for k in range(eid.shape[1]):
        gates = gates + jnp.where(eid[:, k : k + 1] == lane - n_node, gw[:, k : k + 1].astype(F32), 0.0)
    before = (lax.broadcasted_iota(jnp.int32, (rows, rows), 1) < lax.broadcasted_iota(jnp.int32, (rows, rows), 0)).astype(F32)
    rank = jnp.dot(before.astype(BF16), picked.astype(BF16), preferred_element_type=F32)
    slot = jnp.where(picked > 0.5, rank + (y * cap).astype(F32), -1.0)
    meta = jnp.where(lane < n_node, slot, gates).astype(BF16)
    ym[y] = meta.reshape(tr, 8, 128)

    pl.semaphore_wait(barrier, n_node - 1 + n_loc - 1)

    def y1(kind, d):
        p = lax.rem(y + d, n_loc)
        src = (ym.at[y], tA.at[p], yb.at[y])[kind]
        dst = (ym.at[y], ya.at[y], yb.at[y])[kind]
        return ycopy(src, dst, y_s.at[kind, d], y_r.at[kind, d], p)

    def y1_in(kind, d):
        p = lax.rem(y + n_loc - d, n_loc)
        dst = (ym.at[p], ya.at[p], yb.at[p])[kind]
        return ycopy(dst, dst, y_s.at[kind, d], y_r.at[kind, d], p)

    for d in (1, 3, 2):
        y1(0, d).start()
    for c in tcs:
        c.wait()
    for d in (2, 1, 3):
        y1(1, d).start()
    for d in (2, 1, 3):
        y1(2, d).start()
    for c in ws:
        c.start()

    def gray(k):
        return k + (k // 2) * (1 - 2 * lax.rem(k, 2))

    for d in (1, 3, 2):
        y1_in(0, d).wait_recv()
    mall = ym[...].reshape(toks, 128)
    ex = (lax.broadcasted_iota(jnp.int32, (n_node, blk, 128), 0) == lax.broadcasted_iota(jnp.int32, (n_node, blk, 128), 2)).astype(F32)
    ex = ex.reshape(slots, 128).astype(BF16)
    pick = lax.dot_general(ex, mall, (((1,), (1,)), ((), ())), preferred_element_type=F32)
    want = lax.broadcasted_iota(jnp.int32, (n_node, blk, toks), 1).astype(F32).reshape(slots, toks)
    sel[...] = jnp.where(pick == want, 1.0, 0.0).astype(BF16)
    pickT = lax.dot_general(mall, ex, (((1,), (1,)), ((), ())), preferred_element_type=F32)
    ln = lax.broadcasted_iota(jnp.int32, (toks, slots), 1).astype(F32)
    wantT = ln - blk * jnp.floor((ln + 0.5) * (1.0 / blk))
    selT[...] = jnp.where(pickT == wantT, 1.0, 0.0).astype(BF16)

    def a_out(m):
        return ncopy(sendA.at[pl.ds(m * cpn, cpn)], xa.at[y, pl.ds(me * cpn, cpn)], a_s.at[m], a_r.at[me], m)

    def a_in(m):
        dst = xa.at[y, pl.ds(m * cpn, cpn)]
        return ncopy(dst, dst, a_s.at[m], a_r.at[m], m)

    def b_out(m):
        return ncopy(sendB.at[pl.ds(m * cpn, cpn)], xb.at[pl.ds(me * cpn, cpn)], b_s.at[m], b_r.at[me], m)

    def b_in(m):
        dst = xb.at[pl.ds(m * cpn, cpn)]
        return ncopy(dst, dst, b_s.at[m], b_r.at[m], m)

    def each(g, fn):
        @pl.loop(0, gn)
        def _(j):
            m = g * gn + lax.rem(me + j, gn)

            @pl.when(m != me)
            def _():
                fn(m)

    for d in (1, 3, 2):
        y1_in(1, d).wait_recv()

    @pl.loop(0, ng)
    def _(k):
        g = lax.rem(mx + gray(k), ng)
        rs_ = pl.ds(pl.multiple_of(g * gr, 16), gr)
        val = jnp.dot(sel[rs_, :], ya[...].reshape(toks, a), preferred_element_type=F32)
        sendA[pl.ds(g * gc, gc)] = val.astype(BF16).reshape(gc, 8, a)
        each(g, lambda m: a_out(m).start())

    xa[y, pl.ds(me * cpn, cpn)] = sendA[pl.ds(me * cpn, cpn)]

    for d in (1, 3, 2):
        y1_in(2, d).wait_recv()

    @pl.loop(0, ng)
    def _(k):
        g = lax.rem(mx + gray(k), ng)
        rs_ = pl.ds(pl.multiple_of(g * gr, 16), gr)
        val = jnp.dot(sel[rs_, :], ym[...].reshape(toks, 128), preferred_element_type=F32)
        sendB[pl.ds(g * gc, gc), :, pl.ds(b, 128)] = val.astype(BF16).reshape(gc, 8, 128)
        val = jnp.dot(sel[rs_, :], yb[...].reshape(toks, b), preferred_element_type=F32)
        sendB[pl.ds(g * gc, gc), :, pl.ds(0, b)] = val.astype(BF16).reshape(gc, 8, b)
        each(g, lambda m: b_out(m).start())

    xb[pl.ds(me * cpn, cpn)] = sendB[pl.ds(me * cpn, cpn)]

    lo = pl.ds(0, half)
    hi = pl.ds(half, half)

    def ag(kind, k, g):
        gs = pl.ds(g * gc, gc)
        if kind == 0:
            src, p = xa.at[y, gs], yu
        elif kind == 1:
            src, p = xa.at[y, gs], yd
        elif kind == 2:
            src, p = xa.at[yd, gs, :, lo], yu
        else:
            src, p = xa.at[yu, gs, :, hi], yd
        return ycopy(src, src, ag_s.at[kind, k], ag_r.at[kind, k], p)

    def ag_in(kind, k, g):
        gs = pl.ds(g * gc, gc)
        dst = (xa.at[yd, gs], xa.at[yu, gs], xa.at[yo, gs, :, lo], xa.at[yo, gs, :, hi])[kind]
        return ycopy(dst, dst, ag_s.at[kind, k], ag_r.at[kind, k], y)

    def rs(kind, k, g):
        gs = pl.ds(g * gc, gc)
        if kind == 0:
            src, dst, p = pa.at[yo, gs, :, lo], r1d.at[gs], yu
        elif kind == 1:
            src, dst, p = pa.at[yo, gs, :, hi], r1u.at[gs], yd
        elif kind == 2:
            src, dst, p = pa.at[yu, gs], r2d.at[gs], yu
        else:
            src, dst, p = pa.at[yd, gs], r2u.at[gs], yd
        return ycopy(src, dst, rs_s.at[kind, k], rs_r.at[kind, k], p)

    def rs_in(kind, k, g):
        gs = pl.ds(g * gc, gc)
        dst = (r1d, r1u, r2d, r2u)[kind].at[gs]
        return ycopy(dst, dst, rs_s.at[kind, k], rs_r.at[kind, k], y)

    def ra_out(m):
        return ncopy(acc.at[pl.ds(m * cpn, cpn)], retA.at[pl.ds(me * cpn, cpn)], ra_s.at[m], ra_r.at[me], m)

    def ra_in(m):
        dst = retA.at[pl.ds(m * cpn, cpn)]
        return ncopy(dst, dst, ra_s.at[m], ra_r.at[m], m)

    def rb_out(m):
        return ncopy(pb.at[pl.ds(m * cpn, cpn)], retB.at[pl.ds(me * cpn, cpn)], rb_s.at[m], rb_r.at[me], m)

    def rb_in(m):
        dst = retB.at[pl.ds(m * cpn, cpn)]
        return ncopy(dst, dst, rb_s.at[m], rb_r.at[m], m)

    for c in ws:
        c.wait()

    btile = 512

    def experts(g):
        gs = pl.ds(g * gc, gc)
        glane = lax.broadcasted_iota(jnp.int32, (gr, 128), 1)
        gall = xb[gs, :, pl.ds(b, 128)].astype(F32).reshape(gr, 128)

        @pl.loop(0, n_exp)
        def _(e):
            cs = pl.ds(pl.multiple_of(e * ff, 128), ff)
            v = jnp.zeros((gr, ff), F32)
            for s in range(n_loc):
                v = v + jnp.dot(xa[s, gs].reshape(gr, a), upv[pl.ds(s * a, a), cs], preferred_element_type=F32)
            v = v + jnp.dot(xb[gs, :, pl.ds(0, b)].reshape(gr, b), upv[pl.ds(n_loc * a, b), cs], preferred_element_type=F32)
            gate = jnp.sum(jnp.where(glane == n_node + me * n_exp + e, gall, 0.0), axis=1, keepdims=True)
            hs[:, cs] = (v / (1.0 + jnp.exp(-v)) * gate).astype(BF16)

        @pl.loop(0, n_loc)
        def _(s):
            v = jnp.dot(hs[...], dnv[:, pl.ds(pl.multiple_of(s * a, 128), a)], preferred_element_type=F32)
            pa[s, gs] = v.astype(BF16).reshape(gc, 8, a)

        @pl.loop(0, b // btile)
        def _(t):
            v = jnp.dot(hs[...], dnv[:, pl.ds(pl.multiple_of(n_loc * a + t * btile, 128), btile)], preferred_element_type=F32)
            pb[gs, :, pl.ds(pl.multiple_of(t * btile, 128), btile)] = v.astype(BF16).reshape(gc, 8, btile)

    def group_in(k):
        return lax.rem(mx + ng - gray(k), ng)

    @pl.loop(0, ng + 5)
    def _(i):
        @pl.when(i < ng)
        def _():
            k = i
            g = group_in(k)
            each(g, lambda m: a_in(m).wait_recv())
            ag(0, k, g).start()
            ag(1, k, g).start()

        @pl.when(jnp.logical_and(i >= 1, i < ng + 1))
        def _():
            k = i - 1
            g = group_in(k)
            ag_in(0, k, g).wait_recv()
            ag(2, k, g).start()
            ag_in(1, k, g).wait_recv()
            ag(3, k, g).start()

        @pl.when(jnp.logical_and(i >= 2, i < ng + 2))
        def _():
            k = i - 2
            g = group_in(k)
            each(g, lambda m: b_in(m).wait_recv())
            ag_in(2, k, g).wait_recv()
            ag_in(3, k, g).wait_recv()
            experts(g)
            rs(0, k, g).start()
            rs(1, k, g).start()
            each(g, lambda m: rb_out(m).start())

        @pl.when(jnp.logical_and(i >= 3, i < ng + 3))
        def _():
            k = i - 3
            g = group_in(k)
            gs = pl.ds(g * gc, gc)
            rs_in(0, k, g).wait_recv()
            pa[yu, gs, :, lo] = (pa[yu, gs, :, lo].astype(F32) + r1d[gs].astype(F32)).astype(BF16)
            rs(2, k, g).start()
            rs_in(1, k, g).wait_recv()
            pa[yd, gs, :, hi] = (pa[yd, gs, :, hi].astype(F32) + r1u[gs].astype(F32)).astype(BF16)
            rs(3, k, g).start()

        @pl.when(jnp.logical_and(i >= 4, i < ng + 4))
        def _():
            k = i - 4
            g = group_in(k)
            gs = pl.ds(g * gc, gc)
            rs_in(2, k, g).wait_recv()
            rs_in(3, k, g).wait_recv()
            acc[gs] = (pa[y, gs].astype(F32) + r2d[gs].astype(F32) + r2u[gs].astype(F32)).astype(BF16)
            each(g, lambda m: ra_out(m).start())

    mine = pl.ds(me * cpn, cpn)
    retB[mine] = pb[mine]
    retA[mine] = acc[mine]

    def fin(kind, d):
        p = lax.rem(y + d, n_loc)
        return ycopy((fA, fB)[kind].at[p], (oA, oB)[kind].at[y], f_s.at[kind, d], f_r.at[kind, d], p)

    def fin_in(kind, d):
        p = lax.rem(y + n_loc - d, n_loc)
        dst = (oA, oB)[kind].at[p]
        return ycopy(dst, dst, f_s.at[kind, d], f_r.at[kind, d], p)

    for k in range(ng):
        each(lax.rem(mx + gray(k), ng), lambda m: rb_in(m).wait_recv())

    @pl.loop(0, b // btile)
    def _(t):
        cs = pl.ds(pl.multiple_of(t * btile, 128), btile)
        v = jnp.dot(selT[...], retB[:, :, cs].reshape(slots, btile), preferred_element_type=F32)
        fB[:, :, :, cs] = v.astype(BF16).reshape(n_loc, tr, 8, btile)

    for d in (2, 1, 3):
        fin(1, d).start()
    for k in range(ng):
        each(lax.rem(mx + gray(k), ng), lambda m: ra_in(m).wait_recv())
    v = jnp.dot(selT[...], retA[...].reshape(slots, a), preferred_element_type=F32)
    fA[...] = v.astype(BF16).reshape(n_loc, tr, 8, a)
    for d in (2, 1, 3):
        fin(0, d).start()
    oA[y] = fA[y]
    oB[y] = fB[y]
    for d in (1, 3, 2):
        fin_in(1, d).wait_recv()
    tot = oB[0].astype(F32)
    for s in range(1, n_loc):
        tot = tot + oB[s].astype(F32)
    out[:, :, pl.ds(n_loc * a, b)] = tot.astype(BF16)
    for d in (1, 3, 2):
        fin_in(0, d).wait_recv()
    for s in range(n_loc):
        out[:, :, pl.ds(s * a, a)] = oA[s]

    for d in range(1, n_loc):
        for kind in range(3):
            y1(kind, d).wait_send()
        for kind in range(2):
            fin(kind, d).wait_send()

    @pl.loop(0, ng)
    def _(k):
        g = group_in(k)
        each(g, lambda m: (a_out(m).wait_send(), b_out(m).wait_send(), ra_out(m).wait_send(), rb_out(m).wait_send()) and None)
        for kind in range(4):
            ag(kind, k, g).wait_send()
            rs(kind, k, g).wait_send()


def body(tokens, node_ids, expert_ids, gate_weights, up_weight, down_weight):
    rows, d_model = tokens.shape
    n_node, n_loc = lax.axis_size("node"), lax.axis_size("local")
    n_exp, _, ff = up_weight.shape
    cap = node_ids.shape[1] * rows // n_node
    tr = rows // 8
    a = SLICE
    b = d_model - n_loc * a
    nb = n_node * n_loc * cap // 8
    cfg = (n_node, n_loc, cap, n_exp, tr, d_model, ff, a, b)
    slots = nb * 8
    toks = n_loc * rows
    v = lambda *s: pltpu.VMEM(s, BF16)
    dma = lambda *s: pltpu.SemaphoreType.DMA(s)
    scratch = [
        v(n_loc, tr, 8, a),
        v(n_loc, tr, 8, a),
        v(n_loc, tr, 8, b),
        v(n_loc, tr, 8, 128),
        v(slots, toks),
        v(toks, slots),
        v(nb, 8, a),
        v(nb, 8, b + 128),
        v(n_loc, nb, 8, a),
        v(nb, 8, b + 128),
        v(d_model, n_exp * ff),
        v(n_exp * ff, d_model),
        v(slots // 4, n_exp * ff),
        v(n_loc, nb, 8, a),
        v(nb, 8, b),
        v(nb, 8, a // 2),
        v(nb, 8, a // 2),
        v(nb, 8, a),
        v(nb, 8, a),
        v(nb, 8, a),
        v(nb, 8, a),
        v(nb, 8, b),
        v(n_loc, tr, 8, a),
        v(n_loc, tr, 8, b),
        v(n_loc, tr, 8, a),
        v(n_loc, tr, 8, b),
        dma(n_loc + 2),
        dma(2 * n_exp),
        dma(3, n_loc), dma(3, n_loc),
        dma(n_node), dma(n_node),
        dma(n_node), dma(n_node),
        dma(4, 4), dma(4, 4),
        dma(4, 4), dma(4, 4),
        dma(n_node), dma(n_node),
        dma(n_node), dma(n_node),
        dma(2, n_loc), dma(2, n_loc),
    ]
    vm = pl.BlockSpec(memory_space=pltpu.VMEM)
    hbm = pl.BlockSpec(memory_space=pl.ANY)
    out = pl.pallas_call(
        functools.partial(kernel, cfg),
        out_shape=jax.ShapeDtypeStruct((tr, 8, d_model), BF16),
        in_specs=[hbm, vm, vm, vm, hbm, hbm],
        out_specs=vm,
        scratch_shapes=scratch,
        compiler_params=pltpu.CompilerParams(collective_id=0, has_side_effects=True, vmem_limit_bytes=67043328),
    )(tokens.reshape(tr, 8, d_model), node_ids, expert_ids, gate_weights, up_weight, down_weight)
    return out.reshape(rows, d_model)


def solution(mesh):
    in_specs = (
        P(("node", "local"), None),
        P(("node", "local"), None),
        P(("node", "local"), None),
        P(("node", "local"), None),
        P("node", None, "local"),
        P("node", "local", None),
    )
    out_specs = P(("node", "local"), None)
    return jax.shard_map(body, mesh=mesh, in_specs=in_specs, out_specs=out_specs, check_vma=False)
```

time: 325 us -> 171 us (0.53)
  waiting for transfers between devices: 166 us -> 0 us
  Pallas kernels: 0 us -> 165 us
  blocking collectives: 64.4 us -> 0 us
  matrix products: 59.9 us -> 0 us
  between operations: 13.6 us -> 0.01 us
  starting transfers between devices: 7.77 us -> 0 us
  local copies, waits for them, and re-layouts: 11.9 us -> 6.1 us
    pallas_call x0 -> x1, Pallas kernels: none -> 165 us  [body(): pl.pallas_call(functools.partial(kernel, cfg), out_shape=jax.ShapeDtypeSt...]
    reduce_scatter x1 -> x0, waiting for transfers between devices: 77.8 us -> none  [body(): lax.psum_scatter(running.astype(jnp.bfloat16).astype(jnp.float32).astype(...]
    dot_general x6 -> x0, matrix products: 59.9 us -> none  [the longest x3 55.4 us: body(): jnp.dot(scaled, down_weight[expert], preferred_element_type=jnp.float32)]
    all_to_all x2 -> x0, blocking collectives: 54.1 us -> none  [the longest x1 43.4 us: body(): lax.all_to_all(outgoing.reshape(node_count, capacity, model_width), 'node...]
    all_gather x1 -> x0, waiting for transfers between devices: 53.9 us -> none  [body(): lax.all_gather(arrived, 'local', axis=0, tiled=True)]
    all_to_all x1 -> x0, waiting for transfers between devices: 33.8 us -> none  [body(): lax.all_to_all(summed.reshape(node_count, capacity, model_width), 'node',...]
    reshape x7 -> x0, local copies, waits for them, and re-layouts: 11.2 us -> none  [the longest x1 4.18 us: body(): summed.reshape(node_count, capacity, model_width)]
    all_gather x1 -> x0, blocking collectives: 10.3 us -> none  [body(): lax.all_gather(arrived_gates, 'local', axis=0, tiled=True)]
  transfers between devices with their start and end apart: 3 -> 0, of which waited for: 3 -> 0; matrix products, arithmetic and copies ran while one was open for 0% -> 0% of each run, Pallas kernels for 0% -> 0%
where the time goes in v1:
time: 171 us
  Pallas kernels  165 us (96%)
  local copies, waits for them, and re-layouts  6.1 us (4%)
    pallas_call x1, Pallas kernels, body(): pl.pallas_call(functools.partial(kernel, cfg), out_shape=jax.ShapeDtypeSt...  165 us
    unnamed x4, local copies, waits for them, and re-layouts  6.1 us

profile of v1, /device:TPU:1, one launch (start us, length us, event | category | flops | bytes accessed | tf_op | source)
XLA Modules:
  0.0 171.0 jit_solution(10657285914719300252)
XLA Ops:
  0.0 1.4 copy.9.gw
  1.4 1.4 copy.7.nid
  2.8 1.4 copy.8.eid
  4.1 164.9 %shard_map.64 = bf16[8,8,5120]{2,1,0:T(8,128)(2,1)} custom-call(bf16[8,8,5120]{2,1,0:T(8,128)(2,1)} %bitcast.3, s32[64,3]{1,0:T(8,128)} %copy.7.nid, s32[64,6]{1,0:T(8,128)} %copy.8.eid, bf16[64,6]{1,0:T(8,128)(2,1)} %copy.9.gw, bf16[3,5120,384]{2,1,0:T(8,128)(2,1)} %up.1, bf16[3,384,5120]{2,1,0:T(8,128)(2,1)} %down.1), custom_call_target="tpu_custom_call" | custom-call | tf_op jit(solution)/shard_map/pallas_call | solution.py:420
  169.1 2.0 %copy.11 = bf16[64,5120]{1,0:T(8,128)(2,1)} copy(bf16[64,5120]{1,0:T(8,128)(2,1)} %bitcast.2) | data formatting | bytes 1310720

commit v2 on v0

v2 whole, which is shorter than its diff:
```python
import functools

import jax
import jax.numpy as jnp
from jax import lax
from jax.experimental import pallas as pl
from jax.experimental.pallas import tpu as pltpu
from jax.sharding import PartitionSpec as P

SLICE = 768
F32 = jnp.float32
BF16 = jnp.bfloat16


def kernel(cfg, tok, nid, eid, gw, up, down, out, *scr):
    n_node, n_loc, cap, n_exp, tr, ff, a, b = cfg
    (tA, yb, ym, selA, selAT, sel, selT, turn, xs, ps, sA, sB, xa, xb, upv, dnv, hs, r1d, r1u, r2d, r2u, retA, retB, fB, oB,
     tok_sem, w_sem, y_s, y_r, x_s, x_r, z_s, z_r, ag_s, ag_r, rs_s, rs_r, rz_s, rz_r, rx_s, rx_r, f_s, f_r) = scr
    rows = tr * 8
    cpn = n_loc * cap // 8
    blk = cpn * 8
    slots = n_node * blk
    ng = 4
    nz = 4
    gn = n_node // ng
    gc = gn * cpn
    gr = gn * blk
    lo_w = (a // 128 + 1) // 2 * 128
    lo = pl.ds(0, lo_w)
    hi = pl.ds(lo_w, a - lo_w)
    toks = n_loc * rows
    hid = n_exp * ff
    btile = 512
    near = (0, 1, 3, 2)

    me = lax.axis_index("node")
    y = lax.axis_index("local")
    mx = me // gn
    q = lax.rem(me, gn)
    mz = q // 2
    mc = lax.rem(q, 2)
    yu = lax.rem(y + 1, n_loc)
    yd = lax.rem(y + n_loc - 1, n_loc)
    yo = lax.rem(y + 2, n_loc)

    def gray(k):
        return k + (k // 2) * (1 - 2 * (k % 2)) if isinstance(k, int) else k + (k // 2) * (1 - 2 * lax.rem(k, 2))

    def group_out(k):
        return lax.rem(mx + gray(k), ng)

    def group_in(k):
        return lax.rem(mx + ng - gray(k), ng)

    def stage(k):
        far = (k + 3) // 4
        return mx * (1 - far) + (ng + k - 1) * far

    def peer_out(p, h):
        return 2 * lax.rem(mz + near[p], nz) + lax.rem(mc + h, 2)

    def cells(n):
        return pl.ds(n * cpn, cpn)

    def ncopy(src, dst, ss, rs, m):
        return pltpu.make_async_remote_copy(src, dst, ss, rs, device_id={"node": m}, device_id_type=pl.DeviceIdType.MESH)

    def ycopy(src, dst, ss, rs, p):
        return pltpu.make_async_remote_copy(src, dst, ss, rs, device_id={"local": p}, device_id_type=pl.DeviceIdType.MESH)

    barrier = pltpu.get_barrier_semaphore()
    for d in (2, 1, 3):
        pl.semaphore_signal(barrier, 1, device_id={"local": lax.rem(y + d, n_loc)}, device_id_type=pl.DeviceIdType.MESH)
    for d in (2, 1, 3):
        pl.semaphore_signal(barrier, 1, device_id={"node": lax.rem(mx + d, ng) * gn + q}, device_id_type=pl.DeviceIdType.MESH)
    for d in (4, 5, 3, 2, 6, 7, 1):
        pl.semaphore_signal(barrier, 1, device_id={"node": mx * gn + lax.rem(q + d, gn)}, device_id_type=pl.DeviceIdType.MESH)

    tcs = [pltpu.make_async_copy(tok.at[:, :, pl.ds(s * a, a)], tA.at[s], tok_sem.at[s]) for s in range(n_loc)]
    tcs.append(pltpu.make_async_copy(tok.at[:, :, pl.ds(n_loc * a, b)], yb.at[y], tok_sem.at[n_loc]))
    for c in tcs:
        c.start()
    ws = []
    for e in range(n_exp):
        ws.append(pltpu.make_async_copy(up.at[e], upv.at[:, pl.ds(e * ff, ff)], w_sem.at[e]))
        ws.append(pltpu.make_async_copy(down.at[e], dnv.at[pl.ds(e * ff, ff), :], w_sem.at[n_exp + e]))

    sub = lax.broadcasted_iota(jnp.int32, (128, rows), 0)
    picked = jnp.zeros((128, rows), F32)
    for k in range(nid.shape[0]):
        picked = jnp.where(nid[k : k + 1, :] == sub, 1.0, picked)
    gates = jnp.zeros((128, rows), F32)
    gwf = gw[...].astype(F32)
    for k in range(eid.shape[0]):
        gates = gates + jnp.where(eid[k : k + 1, :] == sub - n_node, gwf[k : k + 1, :], 0.0)
    i0 = lax.broadcasted_iota(jnp.int32, (rows, rows), 0)
    i1 = lax.broadcasted_iota(jnp.int32, (rows, rows), 1)
    before = jnp.where(i0 < i1, 1.0, 0.0).astype(BF16)
    rank = jnp.dot(picked.astype(BF16), before, preferred_element_type=F32)
    metaT = jnp.where(sub < n_node, jnp.where(picked > 0.5, rank, -1.0), gates).astype(BF16)
    eye = jnp.where(i0 == i1, 1.0, 0.0).astype(BF16)
    meta = lax.dot_general(eye, metaT, (((1,), (1,)), ((), ())), preferred_element_type=F32)
    slot_lane = lax.broadcasted_iota(jnp.int32, (rows, 128), 1) < n_node

    def shifted(n):
        return jnp.where(jnp.logical_and(slot_lane, meta > -0.5), meta + n * cap, meta).astype(BF16)

    def placing(mall, ref, refT):
        ex = (lax.broadcasted_iota(jnp.int32, (n_node, blk, 128), 0) == lax.broadcasted_iota(jnp.int32, (n_node, blk, 128), 2)).astype(F32)
        ex = ex.reshape(slots, 128).astype(BF16)
        pick = lax.dot_general(ex, mall, (((1,), (1,)), ((), ())), preferred_element_type=F32)
        want = lax.broadcasted_iota(jnp.int32, (n_node, blk, toks), 1).astype(F32).reshape(slots, toks)
        ref[...] = jnp.where(pick == want, 1.0, 0.0).astype(BF16)
        pickT = lax.dot_general(mall, ex, (((1,), (1,)), ((), ())), preferred_element_type=F32)
        ln = lax.broadcasted_iota(jnp.int32, (toks, slots), 1).astype(F32)
        wantT = ln - blk * jnp.floor((ln + 0.5) * (1.0 / blk))
        refT[...] = jnp.where(pickT == wantT, 1.0, 0.0).astype(BF16)

    ym[y] = shifted(y.astype(F32)).reshape(tr, 8, 128)
    placing(jnp.concatenate([shifted(float(s)) for s in range(n_loc)], axis=0), selA, selAT)
    for c in tcs:
        c.wait()
    for k in range(ng):
        gs = group_out(k)
        v = jnp.dot(selA[pl.ds(pl.multiple_of(gs * gr, 16), gr), :], tA[...].reshape(toks, a), preferred_element_type=F32)
        sA[pl.ds(gs * gc, gc)] = v.astype(BF16).reshape(gc, 8, a)

    with jax.named_scope("barrier"):
        pl.semaphore_wait(barrier, n_loc - 1 + ng - 1 + gn - 1)

    ybuf = (ym, yb)

    def spread_tokens(kind):
        for d in (2, 1, 3):
            p = lax.rem(y + d, n_loc)
            ycopy(ybuf[kind].at[y], ybuf[kind].at[y], y_s.at[kind], y_r.at[kind], p).start()

    def all_tokens(kind):
        ref = ybuf[kind].at[pl.ds(0, n_loc - 1)]
        return ycopy(ref, ref, y_s.at[kind], y_r.at[kind], y)

    spread_tokens(0)
    spread_tokens(1)

    sbuf = (sA, sB)

    def land(kind, n):
        return xa.at[y, cells(n)] if kind == 0 else xb.at[cells(n)]

    def xleg(kind, k, p):
        z = lax.rem(mz + near[p], nz)
        src = sbuf[kind].at[pl.ds((group_out(k) * gn + 2 * z) * cpn, 2 * cpn)]
        dst = sbuf[kind].at[pl.ds((stage(k) * gn + 2 * z) * cpn, 2 * cpn)]
        return ncopy(src, dst, x_s.at[kind, k - 1, p], x_r.at[kind, k - 1, p], group_out(k) * gn + q)

    def zleg(kind, k, p, h):
        to = peer_out(p, h)
        src = sbuf[kind].at[cells(stage(k) * gn + to)]
        return ncopy(src, land(kind, group_in(k) * gn + q), z_s.at[kind, k], z_r.at[kind, k], mx * gn + to)

    def all_forwarded(kind, k):
        dst = xa.at[y, pl.ds(0, (gn - 1) * cpn)] if kind == 0 else xb.at[pl.ds(0, (gn - 1) * cpn)]
        return ncopy(sbuf[kind].at[pl.ds(0, (gn - 1) * cpn)], dst, z_s.at[kind, k], z_r.at[kind, k], me)

    def forward(kind, k, p):
        if k > 0:
            xleg(kind, k, p).wait_recv()
        if p > 0:
            zleg(kind, k, p, 0).start()
        zleg(kind, k, p, 1).start()
        if p == 0:
            n = group_in(k) * gn + q
            if kind == 0:
                xa[y, cells(n)] = sA[cells(stage(k) * gn + q)]
            else:
                xb[cells(n)] = sB[cells(stage(k) * gn + q)]

    def arrived(kind, k):
        all_forwarded(kind, k).wait_recv()

    def near_leg(kind, k):
        for p in range(nz):
            xleg(kind, k, p).start()

    def select(k):
        g = group_out(k)
        pick_rows = sel[pl.ds(pl.multiple_of(g * gr, 16), gr), :]
        gs = pl.ds(g * gc, gc)
        v = jnp.dot(pick_rows, ym[...].reshape(toks, 128), preferred_element_type=F32)
        sB[gs, :, pl.ds(b, 128)] = v.astype(BF16).reshape(gc, 8, 128)
        v = jnp.dot(pick_rows, yb[...].reshape(toks, b), preferred_element_type=F32)
        sB[gs, :, pl.ds(0, b)] = v.astype(BF16).reshape(gc, 8, b)

    def far_leg(kind, *ps):
        for p in ps:
            xleg(kind, 3, p).start()

    def ag(kind, k):
        gs = pl.ds(group_in(k) * gc, gc)
        if kind == 0:
            src, p = xa.at[y, gs], yu
        elif kind == 1:
            src, p = xa.at[y, gs], yd
        elif kind == 2:
            src, p = xa.at[yd, gs, :, lo], yu
        else:
            src, p = xa.at[yu, gs, :, hi], yd
        return ycopy(src, src, ag_s.at[kind, k], ag_r.at[kind, k], p)

    def ag_in(kind, k):
        gs = pl.ds(group_in(k) * gc, gc)
        dst = (xa.at[yd, gs], xa.at[yu, gs], xa.at[yo, gs, :, lo], xa.at[yo, gs, :, hi])[kind]
        return ycopy(dst, dst, ag_s.at[kind, k], ag_r.at[kind, k], y)

    def spread(k):
        with jax.named_scope("spread"):
            arrived(0, k)
            ag(0, k).start()
            ag(1, k).start()

    def spread_far(k):
        with jax.named_scope("spread_far"):
            ag_in(0, k).wait_recv()
            ag(2, k).start()
            ag_in(1, k).wait_recv()
            ag(3, k).start()

    def rs(kind, k):
        gs = pl.ds(group_in(k) * gc, gc)
        if kind == 0:
            src, dst, p = xa.at[yo, gs, :, lo], r1d.at[gs], yu
        elif kind == 1:
            src, dst, p = xa.at[yo, gs, :, hi], r1u.at[gs], yd
        elif kind == 2:
            src, dst, p = xa.at[yu, gs], r2d.at[gs], yu
        else:
            src, dst, p = xa.at[yd, gs], r2u.at[gs], yd
        return ycopy(src, dst, rs_s.at[kind, k], rs_r.at[kind, k], p)

    def rs_in(kind, k):
        dst = (r1d, r1u, r2d, r2u)[kind].at[pl.ds(group_in(k) * gc, gc)]
        return ycopy(dst, dst, rs_s.at[kind, k], rs_r.at[kind, k], y)

    rbuf = (retA, retB)

    def result(kind, n, count):
        n = pl.ds(n * cpn, count * cpn)
        return xa.at[y, n] if kind == 0 else xb.at[n, :, pl.ds(0, b)]

    def rx(kind, k, p):
        z = lax.rem(mz + near[p], nz)
        src = result(kind, group_in(k) * gn + 2 * z, 2)
        dst = rbuf[kind].at[pl.ds((stage(k) * gn + 2 * z) * cpn, 2 * cpn)]
        return ncopy(src, dst, rx_s.at[kind, k - 1, p], rx_r.at[kind, k - 1, p], group_in(k) * gn + q)

    def rz(kind, k, p, h):
        to = peer_out(p, h)
        src = result(kind, mx * gn + to, 1) if k == 0 else rbuf[kind].at[cells(stage(k) * gn + to)]
        dst = rbuf[kind].at[cells(group_out(k) * gn + q)]
        return ncopy(src, dst, rz_s.at[kind, k], rz_r.at[kind, k], mx * gn + to)

    def all_back(kind, k):
        ref = rbuf[kind].at[pl.ds(0, (gn - 1) * cpn)]
        return ncopy(ref, ref, rz_s.at[kind, k], rz_r.at[kind, k], me)

    def back(kind, k, p):
        with jax.named_scope("back%d" % kind):
            if k > 0:
                rx(kind, k, p).wait_recv()
            if p > 0:
                rz(kind, k, p, 0).start()
            rz(kind, k, p, 1).start()
            if p == 0:
                to = cells(group_out(k) * gn + q)
                if k > 0:
                    rbuf[kind][to] = rbuf[kind][cells(stage(k) * gn + q)]
                elif kind == 0:
                    retA[to] = xa[y, to]
                else:
                    retB[to] = xb[to, :, pl.ds(0, b)]

    def sum_far(k):
        gs = pl.ds(group_in(k) * gc, gc)
        with jax.named_scope("sum_far"):
            rs_in(0, k).wait_recv()
            xa[yu, gs, :, lo] = (xa[yu, gs, :, lo].astype(F32) + r1d[gs].astype(F32)).astype(BF16)
            rs(2, k).start()
            rs_in(1, k).wait_recv()
            xa[yd, gs, :, hi] = (xa[yd, gs, :, hi].astype(F32) + r1u[gs].astype(F32)).astype(BF16)
            rs(3, k).start()

    def sum_near(k):
        gs = pl.ds(group_in(k) * gc, gc)
        with jax.named_scope("sum_near"):
            rs_in(2, k).wait_recv()
            rs_in(3, k).wait_recv()
            xa[y, gs] = (xa[y, gs].astype(F32) + r2d[gs].astype(F32) + r2u[gs].astype(F32)).astype(BF16)
        for p in (1, 2, 3, 0):
            if k == 0:
                back(0, 0, p)
            else:
                rx(0, k, p).start()

    def experts(k):
        g = group_in(k)
        gs = pl.ds(g * gc, gc)
        glane = lax.broadcasted_iota(jnp.int32, (gr, 128), 1)
        gall = xb[gs, :, pl.ds(b, 128)].astype(F32).reshape(gr, 128)
        gate = [jnp.sum(jnp.where(glane == n_node + me * n_exp + e, gall, 0.0), axis=1, keepdims=True) for e in range(n_exp)]
        planes = jnp.concatenate([xa[s, gs].reshape(gr, a) for s in range(n_loc)], axis=0)
        for s in range(n_loc):
            xs[:, pl.ds(s * a, a)] = jnp.dot(turn[s], planes, preferred_element_type=F32).astype(BF16)
        x = jnp.concatenate([xs[...], xb[gs, :, pl.ds(0, b)].reshape(gr, b)], axis=1)
        for c in range(0, hid, 256):
            w = min(256, hid - c)
            v = jnp.dot(x, upv[:, pl.ds(c, w)], preferred_element_type=F32)
            for j in range(0, w, 128):
                u = v[:, j : j + 128]
                hs[:, pl.ds(c + j, 128)] = (u / (1.0 + jnp.exp(-u)) * gate[(c + j) // ff]).astype(BF16)
        for s in range(n_loc):
            v = jnp.dot(hs[...], dnv[:, pl.ds(s * a, a)], preferred_element_type=F32)
            ps[pl.ds(s * gr, gr), :] = v.astype(BF16)
        for c in range(0, b, btile):
            v = jnp.dot(hs[...], dnv[:, pl.ds(n_loc * a + c, btile)], preferred_element_type=F32)
            xb[gs, :, pl.ds(c, btile)] = v.astype(BF16).reshape(gc, 8, btile)
        for s in range(n_loc):
            v = jnp.dot(turn[s], ps[...], preferred_element_type=F32)
            xa[s, gs] = v.astype(BF16).reshape(gc, 8, a)

    def relay(kind, *ks):
        def steps(p):
            with jax.named_scope("relay%d" % kind):
                for k in ks:
                    forward(kind, k, p)
        return steps

    for k in (1, 2):
        near_leg(0, k)
    for p in range(nz):
        forward(0, 0, p)
    for c in ws:
        c.start()
    place = lax.broadcasted_iota(jnp.int32, (gn, blk, n_loc * gr), 1).astype(F32)
    node_row = lax.broadcasted_iota(jnp.int32, (gn, blk, n_loc * gr), 0).astype(F32)
    column = lax.broadcasted_iota(jnp.int32, (gn, blk, n_loc * gr), 2).astype(F32)
    first = jnp.floor((place + 0.5) * (1.0 / cap)) * (gr - cap) + place + node_row * blk
    for s in range(n_loc):
        turn[s] = jnp.where(column == first + s * cap, 1.0, 0.0).reshape(gr, n_loc * gr).astype(BF16)
    with jax.named_scope("wait_meta"):
        all_tokens(0).wait_recv()
    placing(ym[...].reshape(toks, 128), sel, selT)
    for p in range(nz):
        relay(0, 1, 2)(p)
    far_leg(0, 0, 1, 2, 3)
    spread(0)
    with jax.named_scope("wait_yB"):
        all_tokens(1).wait_recv()
    for k in (1, 2):
        select(k)
        near_leg(1, k)
    select(0)
    for p in range(nz):
        forward(1, 0, p)
    select(3)
    for p in range(nz):
        relay(0, 3)(p)
    spread(1)
    spread_far(0)
    relay(1, 1, 2)(0)
    spread(2)
    relay(1, 1, 2)(1)
    spread_far(1)
    relay(1, 1, 2)(2)
    spread(3)
    relay(1, 1, 2)(3)
    far_leg(1, 0, 1, 2, 3)
    for c in ws:
        c.wait()

    def ready(k):
        with jax.named_scope("ready_b"):
            arrived(1, k)
        with jax.named_scope("ready_a"):
            ag_in(2, k).wait_recv()
            ag_in(3, k).wait_recv()
            for kind in range(4):
                ag(kind, k).wait_send()

    def after(k):
        rs(0, k).start()
        rs(1, k).start()
        for p in (1, 2, 3, 0):
            if k == 0:
                back(1, 0, p)
            else:
                rx(1, k, p).start()

    @pl.loop(0, ng)
    def _(i):
        for k in range(ng):
            @pl.when(i == k)
            def _():
                ready(k)

        with jax.named_scope("experts"):
            experts(i)

        @pl.when(i == 0)
        def _():
            spread_far(2)
            after(0)
            relay(1, 3)(0)
            relay(1, 3)(1)

        @pl.when(i == 1)
        def _():
            after(1)
            spread_far(3)
            relay(1, 3)(2)
            relay(1, 3)(3)
            sum_far(0)

        @pl.when(i == 2)
        def _():
            after(2)
            sum_far(1)

        @pl.when(i == 3)
        def _():
            after(3)

    sum_near(0)
    sum_far(2)
    back(1, 1, 0)
    back(1, 1, 1)
    back(1, 1, 2)
    sum_near(1)
    back(1, 2, 0)
    back(1, 1, 3)
    back(1, 2, 1)
    sum_far(3)
    back(1, 2, 2)
    back(1, 2, 3)
    sum_near(2)
    back(1, 3, 0)
    back(1, 3, 1)
    sum_near(3)
    back(1, 3, 2)
    back(1, 3, 3)
    for p in range(nz):
        back(0, 1, p)

    def fin_all():
        return ycopy(fB.at[pl.ds(0, n_loc - 1)], oB.at[pl.ds(0, n_loc - 1)], f_s.at[0], f_r.at[0], y)

    def returned(kind):
        with jax.named_scope("returned%d" % kind):
            for k in range(ng):
                all_back(kind, k).wait_recv()

    returned(1)
    for c in range(0, b, btile):
        cs = pl.ds(c, btile)
        v = jnp.dot(selT[...], retB[pl.ds(0, slots // 8), :, cs].reshape(slots, btile), preferred_element_type=F32)
        fB[:, :, :, cs] = v.astype(BF16).reshape(n_loc, tr, 8, btile)
    for d in (2, 1, 3):
        p = lax.rem(y + d, n_loc)
        ycopy(fB.at[p], oB.at[y], f_s.at[0], f_r.at[0], p).start()
    oB[y] = fB[y]
    for k in (2, 3):
        for p in range(nz):
            back(0, k, p)
    with jax.named_scope("wait_finB"):
        fin_all().wait_recv()
    tot = oB[0].astype(F32)
    for s in range(1, n_loc):
        tot = tot + oB[s].astype(F32)
    out[:, :, pl.ds(n_loc * a, b)] = tot.astype(BF16)
    returned(0)
    v = jnp.dot(selAT[...], retA[pl.ds(0, slots // 8)].reshape(slots, a), preferred_element_type=F32)
    v = v.astype(BF16).reshape(n_loc, tr, 8, a)
    for s in range(n_loc):
        out[:, :, pl.ds(s * a, a)] = v[s]

    with jax.named_scope("drain"):
        fin_all().wait_send()
        for kind in range(2):
            all_tokens(kind).wait_send()
            for k in range(ng):
                all_forwarded(kind, k).wait_send()
                all_back(kind, k).wait_send()
                for p in range(nz):
                    if k > 0:
                        xleg(kind, k, p).wait_send()
                        rx(kind, k, p).wait_send()
        for k in range(ng):
            for kind in range(4):
                rs(kind, k).wait_send()


def body(tokens, node_ids, expert_ids, gate_weights, up_weight, down_weight):
    rows, d_model = tokens.shape
    n_node, n_loc = lax.axis_size("node"), lax.axis_size("local")
    n_exp, _, ff = up_weight.shape
    cap = node_ids.shape[1] * rows // n_node
    tr = rows // 8
    a = SLICE
    b = d_model - n_loc * a
    nb = n_node * n_loc * cap // 8
    cfg = (n_node, n_loc, cap, n_exp, tr, ff, a, b)
    slots = nb * 8
    toks = n_loc * rows
    v = lambda *s: pltpu.VMEM(s, BF16)
    dma = lambda *s: pltpu.SemaphoreType.DMA(s)
    two_legs = nb // 4 * 7
    lo_w = (a // 128 + 1) // 2 * 128
    scratch = [
        v(n_loc, tr, 8, a),
        v(n_loc, tr, 8, b),
        v(n_loc, tr, 8, 128),
        v(slots, toks),
        v(toks, slots),
        v(slots, toks),
        v(toks, slots),
        v(n_loc, slots // 4, slots),
        v(slots // 4, n_loc * a),
        v(slots, a),
        v(two_legs, 8, a),
        v(two_legs, 8, b + 128),
        v(n_loc, nb, 8, a),
        v(nb, 8, b + 128),
        v(d_model, n_exp * ff),
        v(n_exp * ff, d_model),
        v(slots // 4, n_exp * ff),
        v(nb, 8, lo_w),
        v(nb, 8, a - lo_w),
        v(nb, 8, a),
        v(nb, 8, a),
        v(two_legs, 8, a),
        v(two_legs, 8, b),
        v(n_loc, tr, 8, b),
        v(n_loc, tr, 8, b),
        dma(n_loc + 1),
        dma(2 * n_exp),
        dma(2), dma(2),
        dma(2, 3, 4), dma(2, 3, 4),
        dma(2, 4), dma(2, 4),
        dma(4, 4), dma(4, 4),
        dma(4, 4), dma(4, 4),
        dma(2, 4), dma(2, 4),
        dma(2, 3, 4), dma(2, 3, 4),
        dma(1), dma(1),
    ]
    vm = pl.BlockSpec(memory_space=pltpu.VMEM)
    hbm = pl.BlockSpec(memory_space=pl.ANY)
    out = pl.pallas_call(
        functools.partial(kernel, cfg),
        out_shape=jax.ShapeDtypeStruct((tr, 8, d_model), BF16),
        in_specs=[hbm, vm, vm, vm, hbm, hbm],
        out_specs=vm,
        scratch_shapes=scratch,
        compiler_params=pltpu.CompilerParams(collective_id=0, has_side_effects=True, vmem_limit_bytes=67043328),
    )(tokens.reshape(tr, 8, d_model), node_ids.T, expert_ids.T, gate_weights.T, up_weight, down_weight)
    return out.reshape(rows, d_model)


def solution(mesh):
    in_specs = (
        P(("node", "local"), None),
        P(("node", "local"), None),
        P(("node", "local"), None),
        P(("node", "local"), None),
        P("node", None, "local"),
        P("node", "local", None),
    )
    out_specs = P(("node", "local"), None)
    return jax.shard_map(body, mesh=mesh, in_specs=in_specs, out_specs=out_specs, check_vma=False)
```

time: 325 us -> 139 us (0.43)
  waiting for transfers between devices: 166 us -> 0 us
  Pallas kernels: 0 us -> 136 us
  blocking collectives: 64.4 us -> 0 us
  matrix products: 59.9 us -> 0 us
  between operations: 13.6 us -> 0.01 us
  local copies, waits for them, and re-layouts: 11.9 us -> 1.97 us
  starting transfers between devices: 7.77 us -> 0 us
    pallas_call x0 -> x1, Pallas kernels: none -> 136 us  [body(): pl.pallas_call(functools.partial(kernel, cfg), out_shape=jax.ShapeDtypeSt...]
    reduce_scatter x1 -> x0, waiting for transfers between devices: 77.8 us -> none  [body(): lax.psum_scatter(running.astype(jnp.bfloat16).astype(jnp.float32).astype(...]
    dot_general x6 -> x0, matrix products: 59.9 us -> none  [the longest x3 55.4 us: body(): jnp.dot(scaled, down_weight[expert], preferred_element_type=jnp.float32)]
    all_to_all x2 -> x0, blocking collectives: 54.1 us -> none  [the longest x1 43.4 us: body(): lax.all_to_all(outgoing.reshape(node_count, capacity, model_width), 'node...]
    all_gather x1 -> x0, waiting for transfers between devices: 53.9 us -> none  [body(): lax.all_gather(arrived, 'local', axis=0, tiled=True)]
    all_to_all x1 -> x0, waiting for transfers between devices: 33.8 us -> none  [body(): lax.all_to_all(summed.reshape(node_count, capacity, model_width), 'node',...]
    reshape x7 -> x0, local copies, waits for them, and re-layouts: 11.2 us -> none  [the longest x1 4.18 us: body(): summed.reshape(node_count, capacity, model_width)]
    all_gather x1 -> x0, blocking collectives: 10.3 us -> none  [body(): lax.all_gather(arrived_gates, 'local', axis=0, tiled=True)]
  transfers between devices with their start and end apart: 3 -> 0, of which waited for: 3 -> 0; matrix products, arithmetic and copies ran while one was open for 0% -> 0% of each run, Pallas kernels for 0% -> 0%
where the time goes in v2:
time: 139 us; the launch traced here: 138 us
  Pallas kernels  136 us (98%)
  local copies, waits for them, and re-layouts  1.97 us (1%)
    pallas_call x1, Pallas kernels, body(): pl.pallas_call(functools.partial(kernel, cfg), out_shape=jax.ShapeDtypeSt...  136 us

profile of v2, /device:TPU:1, one launch (start us, length us, event | category | flops | bytes accessed | tf_op | source)
XLA Modules:
  0.0 138.3 jit_solution(5306811918086214300)
XLA Ops:
  0.0 136.4 %shard_map.64 = bf16[8,8,5120]{2,1,0:T(8,128)(2,1)} custom-call(bf16[8,8,5120]{2,1,0:T(8,128)(2,1)} %bitcast.6, s32[3,64]{1,0:T(4,128)} %bitcast.8, s32[6,64]{1,0:T(8,128)} %bitcast.7, bf16[6,64]{1,0:T(8,128)(2,1)} %bitcast.9, bf16[3,5120,384]{2,1,0:T(8,128)(2,1)} %up.1, bf16[3,384,5120]{2,1,0:T(8,128)(2,1)} %down.1), custom_call_target="tpu_custom_call" | custom-call | tf_op jit(solution)/shard_map/pallas_call | solution.py:556
  136.4 2.0 %copy.8 = bf16[64,5120]{1,0:T(8,128)(2,1)} copy(bf16[64,5120]{1,0:T(8,128)(2,1)} %bitcast.5) | data formatting | bytes 1310720

commit v3 on v2

--- a/solution.py
+++ b/solution.py
@@ -7,7 +7,7 @@
 from jax.experimental.pallas import tpu as pltpu
 from jax.sharding import PartitionSpec as P
 
-SLICE = 768
+SLICE = 896
 F32 = jnp.float32
 BF16 = jnp.bfloat16
 
@@ -387,8 +387,9 @@
                 ag(kind, k).wait_send()
 
     def after(k):
-        rs(0, k).start()
-        rs(1, k).start()
+        if k > 0:
+            rs(0, k).start()
+            rs(1, k).start()
         for p in (1, 2, 3, 0):
             if k == 0:
                 back(1, 0, p)
@@ -410,45 +411,46 @@
             spread_far(2)
             after(0)
             relay(1, 3)(0)
-            relay(1, 3)(1)
 
         @pl.when(i == 1)
         def _():
             after(1)
             spread_far(3)
+            relay(1, 3)(1)
             relay(1, 3)(2)
             relay(1, 3)(3)
-            sum_far(0)
 
         @pl.when(i == 2)
         def _():
             after(2)
             sum_far(1)
+            rs(0, 0).start()
+            rs(1, 0).start()
+            back(1, 1, 0)
+            back(1, 1, 1)
+            back(1, 1, 2)
 
         @pl.when(i == 3)
         def _():
             after(3)
 
-    sum_near(0)
     sum_far(2)
-    back(1, 1, 0)
-    back(1, 1, 1)
-    back(1, 1, 2)
+    back(1, 1, 3)
+    back(1, 2, 0)
+    back(1, 2, 1)
     sum_near(1)
-    back(1, 2, 0)
-    back(1, 1, 3)
-    back(1, 2, 1)
-    sum_far(3)
     back(1, 2, 2)
     back(1, 2, 3)
+    back(1, 3, 0)
+    sum_far(3)
+    back(1, 3, 1)
+    back(1, 3, 2)
     sum_near(2)
-    back(1, 3, 0)
-    back(1, 3, 1)
+    sum_far(0)
+    back(1, 3, 3)
+    for p in range(nz):
+        back(0, 1, p)
     sum_near(3)
-    back(1, 3, 2)
-    back(1, 3, 3)
-    for p in range(nz):
-        back(0, 1, p)
 
     def fin_all():
         return ycopy(fB.at[pl.ds(0, n_loc - 1)], oB.at[pl.ds(0, n_loc - 1)], f_s.at[0], f_r.at[0], y)
@@ -467,9 +469,11 @@
         p = lax.rem(y + d, n_loc)
         ycopy(fB.at[p], oB.at[y], f_s.at[0], f_r.at[0], p).start()
     oB[y] = fB[y]
-    for k in (2, 3):
-        for p in range(nz):
-            back(0, k, p)
+    for p in range(nz):
+        back(0, 2, p)
+    sum_near(0)
+    for p in range(nz):
+        back(0, 3, p)
     with jax.named_scope("wait_finB"):
         fin_all().wait_recv()
     tot = oB[0].astype(F32)

time: 139 us -> 132 us (0.950)
  Pallas kernels: 136 us -> 130 us
    pallas_call x1, Pallas kernels: 136 us -> 130 us  [body(): pl.pallas_call(functools.partial(kernel, cfg), out_shape=jax.ShapeDtypeSt...]
where the time goes in v3:
time: 132 us
  Pallas kernels  130 us (98%)
  local copies, waits for them, and re-layouts  1.97 us (1%)
    pallas_call x1, Pallas kernels, body(): pl.pallas_call(functools.partial(kernel, cfg), out_shape=jax.ShapeDtypeSt...  130 us

profile of v3, /device:TPU:1, one launch (start us, length us, event | category | flops | bytes accessed | tf_op | source)
XLA Modules:
  0.0 132.2 jit_solution(6478014858546888059)
XLA Ops:
  0.0 130.3 %shard_map.64 = bf16[8,8,5120]{2,1,0:T(8,128)(2,1)} custom-call(bf16[8,8,5120]{2,1,0:T(8,128)(2,1)} %bitcast.6, s32[3,64]{1,0:T(4,128)} %bitcast.8, s32[6,64]{1,0:T(8,128)} %bitcast.7, bf16[6,64]{1,0:T(8,128)(2,1)} %bitcast.9, bf16[3,5120,384]{2,1,0:T(8,128)(2,1)} %up.1, bf16[3,384,5120]{2,1,0:T(8,128)(2,1)} %down.1), custom_call_target="tpu_custom_call" | custom-call | tf_op jit(solution)/shard_map/pallas_call | solution.py:560
  130.3 2.0 %copy.8 = bf16[64,5120]{1,0:T(8,128)(2,1)} copy(bf16[64,5120]{1,0:T(8,128)(2,1)} %bitcast.5) | data formatting | bytes 1310720

commit v4 on v3

--- a/solution.py
+++ b/solution.py
@@ -14,7 +14,7 @@
 
 def kernel(cfg, tok, nid, eid, gw, up, down, out, *scr):
     n_node, n_loc, cap, n_exp, tr, ff, a, b = cfg
-    (tA, yb, ym, selA, selAT, sel, selT, turn, xs, ps, sA, sB, xa, xb, upv, dnv, hs, r1d, r1u, r2d, r2u, retA, retB, fB, oB,
+    (tA, yb, ym, selA, selAT, sel, selT, turn, xs, ps, sA, sB, xa, xb, upv, dnv, hs, r1, r2d, r2u, retA, retB, fB, oB,
      tok_sem, w_sem, y_s, y_r, x_s, x_r, z_s, z_r, ag_s, ag_r, rs_s, rs_r, rz_s, rz_r, rx_s, rx_r, f_s, f_r) = scr
     rows = tr * 8
     cpn = n_loc * cap // 8
@@ -25,9 +25,6 @@
     gn = n_node // ng
     gc = gn * cpn
     gr = gn * blk
-    lo_w = (a // 128 + 1) // 2 * 128
-    lo = pl.ds(0, lo_w)
-    hi = pl.ds(lo_w, a - lo_w)
     toks = n_loc * rows
     hid = n_exp * ff
     btile = 512
@@ -58,6 +55,9 @@
 
     def peer_out(p, h):
         return 2 * lax.rem(mz + near[p], nz) + lax.rem(mc + h, 2)
+
+    def half(k, h):
+        return pl.ds(group_in(k) * gc + h * (gc // 2), gc // 2)
 
     def cells(n):
         return pl.ds(n * cpn, cpn)
@@ -202,14 +202,14 @@
         elif kind == 1:
             src, p = xa.at[y, gs], yd
         elif kind == 2:
-            src, p = xa.at[yd, gs, :, lo], yu
+            src, p = xa.at[yd, half(k, 0)], yu
         else:
-            src, p = xa.at[yu, gs, :, hi], yd
+            src, p = xa.at[yu, half(k, 1)], yd
         return ycopy(src, src, ag_s.at[kind, k], ag_r.at[kind, k], p)
 
     def ag_in(kind, k):
         gs = pl.ds(group_in(k) * gc, gc)
-        dst = (xa.at[yd, gs], xa.at[yu, gs], xa.at[yo, gs, :, lo], xa.at[yo, gs, :, hi])[kind]
+        dst = (xa.at[yd, gs], xa.at[yu, gs], xa.at[yo, half(k, 0)], xa.at[yo, half(k, 1)])[kind]
         return ycopy(dst, dst, ag_s.at[kind, k], ag_r.at[kind, k], y)
 
     def spread(k):
@@ -228,9 +228,9 @@
     def rs(kind, k):
         gs = pl.ds(group_in(k) * gc, gc)
         if kind == 0:
-            src, dst, p = xa.at[yo, gs, :, lo], r1d.at[gs], yu
+            src, dst, p = xa.at[yo, half(k, 0)], r1.at[half(k, 0)], yu
         elif kind == 1:
-            src, dst, p = xa.at[yo, gs, :, hi], r1u.at[gs], yd
+            src, dst, p = xa.at[yo, half(k, 1)], r1.at[half(k, 1)], yd
         elif kind == 2:
             src, dst, p = xa.at[yu, gs], r2d.at[gs], yu
         else:
@@ -238,7 +238,7 @@
         return ycopy(src, dst, rs_s.at[kind, k], rs_r.at[kind, k], p)
 
     def rs_in(kind, k):
-        dst = (r1d, r1u, r2d, r2u)[kind].at[pl.ds(group_in(k) * gc, gc)]
+        dst = r1.at[half(k, kind)] if kind < 2 else (r2d, r2u)[kind - 2].at[pl.ds(group_in(k) * gc, gc)]
         return ycopy(dst, dst, rs_s.at[kind, k], rs_r.at[kind, k], y)
 
     rbuf = (retA, retB)
@@ -280,13 +280,13 @@
                     retB[to] = xb[to, :, pl.ds(0, b)]
 
     def sum_far(k):
-        gs = pl.ds(group_in(k) * gc, gc)
+        h0, h1 = half(k, 0), half(k, 1)
         with jax.named_scope("sum_far"):
             rs_in(0, k).wait_recv()
-            xa[yu, gs, :, lo] = (xa[yu, gs, :, lo].astype(F32) + r1d[gs].astype(F32)).astype(BF16)
+            xa[yu, h0] = (xa[yu, h0].astype(F32) + r1[h0].astype(F32)).astype(BF16)
             rs(2, k).start()
             rs_in(1, k).wait_recv()
-            xa[yd, gs, :, hi] = (xa[yd, gs, :, hi].astype(F32) + r1u[gs].astype(F32)).astype(BF16)
+            xa[yd, h1] = (xa[yd, h1].astype(F32) + r1[h1].astype(F32)).astype(BF16)
             rs(3, k).start()
 
     def sum_near(k):
@@ -416,6 +416,8 @@
         def _():
             after(1)
             spread_far(3)
+            rs(0, 0).start()
+            rs(1, 0).start()
             relay(1, 3)(1)
             relay(1, 3)(2)
             relay(1, 3)(3)
@@ -424,8 +426,6 @@
         def _():
             after(2)
             sum_far(1)
-            rs(0, 0).start()
-            rs(1, 0).start()
             back(1, 1, 0)
             back(1, 1, 1)
             back(1, 1, 2)
@@ -438,12 +438,12 @@
     back(1, 1, 3)
     back(1, 2, 0)
     back(1, 2, 1)
-    sum_near(1)
     back(1, 2, 2)
     back(1, 2, 3)
+    sum_far(3)
     back(1, 3, 0)
-    sum_far(3)
     back(1, 3, 1)
+    sum_near(1)
     back(1, 3, 2)
     sum_near(2)
     sum_far(0)
@@ -471,9 +471,10 @@
     oB[y] = fB[y]
     for p in range(nz):
         back(0, 2, p)
+    for p in range(nz - 1):
+        back(0, 3, p)
     sum_near(0)
-    for p in range(nz):
-        back(0, 3, p)
+    back(0, 3, nz - 1)
     with jax.named_scope("wait_finB"):
         fin_all().wait_recv()
     tot = oB[0].astype(F32)
@@ -517,7 +518,6 @@
     v = lambda *s: pltpu.VMEM(s, BF16)
     dma = lambda *s: pltpu.SemaphoreType.DMA(s)
     two_legs = nb // 4 * 7
-    lo_w = (a // 128 + 1) // 2 * 128
     scratch = [
         v(n_loc, tr, 8, a),
         v(n_loc, tr, 8, b),
@@ -536,8 +536,7 @@
         v(d_model, n_exp * ff),
         v(n_exp * ff, d_model),
         v(slots // 4, n_exp * ff),
-        v(nb, 8, lo_w),
-        v(nb, 8, a - lo_w),
+        v(nb, 8, a),
         v(nb, 8, a),
         v(nb, 8, a),
         v(two_legs, 8, a),

time: 132 us -> 128 us (0.970)
  Pallas kernels: 130 us -> 126 us
    pallas_call x1, Pallas kernels: 130 us -> 126 us  [body(): pl.pallas_call(functools.partial(kernel, cfg), out_shape=jax.ShapeDtypeSt...]
where the time goes in v4:
time: 128 us
  Pallas kernels  126 us (98%)
  local copies, waits for them, and re-layouts  1.97 us (2%)
    pallas_call x1, Pallas kernels, body(): pl.pallas_call(functools.partial(kernel, cfg), out_shape=jax.ShapeDtypeSt...  126 us

profile of v4, /device:TPU:1, one launch (start us, length us, event | category | flops | bytes accessed | tf_op | source)
XLA Modules:
  0.0 127.7 jit_solution(16242243132525548633)
XLA Ops:
  0.0 125.7 %shard_map.64 = bf16[8,8,5120]{2,1,0:T(8,128)(2,1)} custom-call(bf16[8,8,5120]{2,1,0:T(8,128)(2,1)} %bitcast.6, s32[3,64]{1,0:T(4,128)} %bitcast.8, s32[6,64]{1,0:T(8,128)} %bitcast.7, bf16[6,64]{1,0:T(8,128)(2,1)} %bitcast.9, bf16[3,5120,384]{2,1,0:T(8,128)(2,1)} %up.1, bf16[3,384,5120]{2,1,0:T(8,128)(2,1)} %down.1), custom_call_target="tpu_custom_call" | custom-call | tf_op jit(solution)/shard_map/pallas_call | solution.py:559
  125.7 2.0 %copy.8 = bf16[64,5120]{1,0:T(8,128)(2,1)} copy(bf16[64,5120]{1,0:T(8,128)(2,1)} %bitcast.5) | data formatting | bytes 1310720
